TPU v7x, 128 devices: a whole 4x4x4 slice. The times are simulated.
128 devices in a mesh: row: 8 (over z, y_hi), col: 16 (over x, y_lo, core).
Axes of the slice: x: 4, y: 4 (y_hi: 2, y_lo: 2; y = y_hi * 2 + y_lo), z: 4, core: 2. Of those that a mesh axis runs over, the one named last changes fastest.
Arguments:
- tri_panels: float32 [8192, 8192], P('row', 'col'), may hold values from -1 to 2, as said below
- rhs_rows: float32 [8192, 2048], P(('row', 'col')), may hold values from -6 to 6
Outputs:
- rhs_grid: float32 [8192, 2048], P('row', 'col')
Inputs may be any that keep to these rules, and one draw needn't show every extreme that they name: `tri_panels`: in L's row order the entries above the diagonal are zero and the diagonal entries are positive.
All inputs are finite; a program needn't handle non-finite values.
Results may differ from a plain program's by a relative error of at most 0.00011.
Values sent between devices are 32-bit elements; how exact they have to be, the bound alone decides.
A program may use at most 256 MiB of HBM per device.

v0:
```python
import jax
import jax.numpy as jnp
from jax import lax
from jax.sharding import PartitionSpec as P


def picked(array, axis, root):
    return lax.dynamic_index_in_dim(lax.all_gather(array, axis), root, 0, keepdims=False)


def on_device(tri_panels, rhs_rows):
    row_count = lax.axis_size("row")
    col_count = lax.axis_size("col")
    row_position = lax.axis_index("row")
    col_position = lax.axis_index("col")
    local_rows, block_size = tri_panels.shape
    blocks = local_rows // block_size
    sub_rows = block_size // col_count
    parted = rhs_rows.reshape(blocks, sub_rows, rhs_rows.shape[1])
    state_rhs = lax.all_to_all(parted, "col", split_axis=2, concat_axis=1, tiled=True)
    identity_block = jnp.eye(block_size, dtype=jnp.float32)
    own_pieces = tri_panels.reshape(blocks, block_size, block_size)
    own_diag = lax.dynamic_index_in_dim(own_pieces, col_position // row_count, 0, keepdims=False)
    own_diag = jnp.where(col_position % row_count == row_position, own_diag, identity_block)
    own_inverse = jax.scipy.linalg.solve_triangular(own_diag, identity_block, lower=True)

    def advance(state_rhs, panel_cols, inverse_block, step_index, first_slot):
        count = blocks - first_slot
        owner_row = step_index % row_count
        slot_index = step_index // row_count
        pieces = panel_cols.reshape(count, block_size, block_size)
        current = lax.dynamic_index_in_dim(state_rhs, slot_index, 0, keepdims=False)
        local_solution = jnp.dot(
            inverse_block,
            current,
            precision=lax.Precision.HIGHEST,
            preferred_element_type=jnp.float32,
        )
        solution = picked(local_solution, "row", owner_row)
        stored = jnp.where(row_position == owner_row, solution, current)
        state_rhs = lax.dynamic_update_index_in_dim(state_rhs, stored, slot_index, 0)
        global_block = (first_slot + jnp.arange(count, dtype=jnp.int32)) * row_count + row_position
        product = jnp.einsum("sij,jc->sic", pieces, solution, precision=lax.Precision.HIGHEST)
        trailing = state_rhs[first_slot:]
        trailing = jnp.where(
            (global_block > step_index)[:, None, None], trailing - product, trailing
        )
        if first_slot > 0:
            return jnp.concatenate([state_rhs[:first_slot], trailing], 0)
        return trailing

    group_count = (col_count + row_count - 1) // row_count
    everything, inverses = (
        lax.all_gather(tri_panels, "col", axis=1, tiled=True),
        lax.all_gather(own_inverse, "col", axis=1, tiled=True),
    )
    for first_slot in range(group_count):
        begin_step = first_slot * row_count
        end_step = min(begin_step + row_count, col_count)
        own_rows = everything[first_slot * block_size :]

        def upfront_step(step_index, state_rhs, own_rows=own_rows, first_slot=first_slot):
            panel_cols = lax.dynamic_slice_in_dim(own_rows, step_index * block_size, block_size, 1)
            inverse_block = lax.dynamic_slice_in_dim(
                inverses, step_index * block_size, block_size, 1
            )
            return advance(state_rhs, panel_cols, inverse_block, step_index, first_slot)

        state_rhs = lax.fori_loop(begin_step, end_step, upfront_step, state_rhs)
    return state_rhs.reshape(local_rows, state_rhs.shape[2])


def solution(mesh):
    return jax.shard_map(
        on_device,
        mesh=mesh,
        in_specs=(P("row", "col"), P(("row", "col"), None)),
        out_specs=P("row", "col"),
        check_vma=False,
    )
```

profile of v0, /device:TPU:0, one launch (start us, length us, event | category | flops | bytes accessed | tf_op | source)
XLA Modules:
  0.0 1225.2 jit_solution(3915089604845928567)
XLA Ops:
  9.3 11.6 while.33
  20.9 39.3 %custom-call.4 = f32[4,128,128]{1,2,0:T(8,128)S(1)} custom-call(f32[4,128,128]{2,1,0:T(8,128)S(1)} %get-tuple-element.290), custom_call_target="InvertDiagBlocksLowerTriangular" | custom-call | tf_op jit(solution)/shard_map/jit(_solve_triangular)/triangular_solve | solution.py:25
  71.1 5.6 all-to-all-start
  76.7 14.4 %all-to-all-done = f32[16,1,8192]{2,1,0:T(1,128)S(1)} async-done(((f32[16,1,8192]{2,1,0:T(1,128)}), f32[16,1,8192]{2,1,0:T(1,128)S(1)}, u32[]{:S(2)}, u32[]{:S(2)}) %all-to-all-start) | async-done | bytes 524320 | tf_op jit(solution)/shard_map/all_to_all | solution.py:20
  96.2 91.5 %all-gather.13.cloned.1.call-done = f32[1024,8192]{1,0:T(8,128)} async-done(((f32[1024,512]{1,0:T(8,128)}), f32[1024,8192]{1,0:T(8,128)}) %all-gather.13.cloned.1.call-update) | async-done | bytes 33554448 | tf_op jit(solution)/shard_map/all_gather | solution.py:54
  187.7 11.5 slice.70
  199.2 82.4 %all-gather.11.cloned.1.call-done = f32[512,8192]{1,0:T(8,128)} async-done(((f32[512,512]{1,0:T(8,128)}), f32[512,8192]{1,0:T(8,128)}) %all-gather.11.cloned.1.call-update) | async-done | bytes 16777232 | tf_op jit(solution)/shard_map/all_gather | solution.py:55
  281.6 471.9 %while.31 = (s32[]{:T(128)}, f32[2,512,128]{2,1,0:T(8,128)S(1)}, s32[]{:T(128)}, f32[512,8192]{1,0:T(8,128)}, f32[1024,8192]{1,0:T(8,128)}, /*index=5*/s32[]{:T(...) while((s32[]{:T(128)}, f32[2,512,128]{2,1,0:T(8,128)S(1)}, ...), condition=%wide.region_1.2_spmd, body=%wide.region_0.1_spmd.sunk | while | flops 1208287232 | bytes 17039816 | solution.py:69
  286.3 53.0 %all-gather.15.cloned.1.call-done = f32[4096,128]{1,0:T(8,128)} async-done(((f32[512,128]{1,0:T(8,128)}), f32[4096,128]{1,0:T(8,128)}) %all-gather.15.cloned.1.call-update) | async-done | bytes 2097168 | tf_op jit(solution)/shard_map/while/body/eval_jaxpr/all_gather | solution.py:8
  340.3 3.0 fusion.64
  348.1 49.8 %all-gather.15.cloned.1.call-done = f32[4096,128]{1,0:T(8,128)} async-done(((f32[512,128]{1,0:T(8,128)}), f32[4096,128]{1,0:T(8,128)}) %all-gather.15.cloned.1.call-update) | async-done | bytes 2097168 | tf_op jit(solution)/shard_map/while/body/eval_jaxpr/all_gather | solution.py:8
  398.9 3.0 fusion.64
  406.7 49.8 %all-gather.15.cloned.1.call-done = f32[4096,128]{1,0:T(8,128)} async-done(((f32[512,128]{1,0:T(8,128)}), f32[4096,128]{1,0:T(8,128)}) %all-gather.15.cloned.1.call-update) | async-done | bytes 2097168 | tf_op jit(solution)/shard_map/while/body/eval_jaxpr/all_gather | solution.py:8
  457.5 3.0 fusion.64
  465.3 49.8 %all-gather.15.cloned.1.call-done = f32[4096,128]{1,0:T(8,128)} async-done(((f32[512,128]{1,0:T(8,128)}), f32[4096,128]{1,0:T(8,128)}) %all-gather.15.cloned.1.call-update) | async-done | bytes 2097168 | tf_op jit(solution)/shard_map/while/body/eval_jaxpr/all_gather | solution.py:8
  516.1 3.0 fusion.64
  523.9 49.8 %all-gather.15.cloned.1.call-done = f32[4096,128]{1,0:T(8,128)} async-done(((f32[512,128]{1,0:T(8,128)}), f32[4096,128]{1,0:T(8,128)}) %all-gather.15.cloned.1.call-update) | async-done | bytes 2097168 | tf_op jit(solution)/shard_map/while/body/eval_jaxpr/all_gather | solution.py:8
  574.7 3.0 fusion.64
  582.5 49.8 %all-gather.15.cloned.1.call-done = f32[4096,128]{1,0:T(8,128)} async-done(((f32[512,128]{1,0:T(8,128)}), f32[4096,128]{1,0:T(8,128)}) %all-gather.15.cloned.1.call-update) | async-done | bytes 2097168 | tf_op jit(solution)/shard_map/while/body/eval_jaxpr/all_gather | solution.py:8
  633.3 3.0 fusion.64
  641.1 49.8 %all-gather.15.cloned.1.call-done = f32[4096,128]{1,0:T(8,128)} async-done(((f32[512,128]{1,0:T(8,128)}), f32[4096,128]{1,0:T(8,128)}) %all-gather.15.cloned.1.call-update) | async-done | bytes 2097168 | tf_op jit(solution)/shard_map/while/body/eval_jaxpr/all_gather | solution.py:8
  699.8 49.8 %all-gather.15.cloned.1.call-done = f32[4096,128]{1,0:T(8,128)} async-done(((f32[512,128]{1,0:T(8,128)}), f32[4096,128]{1,0:T(8,128)}) %all-gather.15.cloned.1.call-update) | async-done | bytes 2097168 | tf_op jit(solution)/shard_map/while/body/eval_jaxpr/all_gather | solution.py:8
  750.6 3.0 fusion.64
  753.5 464.0 %while.32 = (s32[]{:T(128)}, f32[2,512,128]{2,1,0:T(8,128)S(1)}, s32[]{:T(128)}, f32[512,8192]{1,0:T(8,128)}, s32[1]{0:T(128)}, /*index=5*/f32[512,8192]{1,0:T(8...) while((s32[]{:T(128)}, f32[2,512,128]{2,1,0:T(8,128)S(1)}, ...), condition=%wide.region_3.4_spmd, body=%wide.region_2.3_spmd.sunk | while | flops 805634048 | bytes 12846105 | solution.py:69
  756.6 51.6 %all-gather.17.cloned.1.call-done = f32[4096,128]{1,0:T(8,128)} async-done(((f32[512,128]{1,0:T(8,128)}), f32[4096,128]{1,0:T(8,128)}) %all-gather.17.cloned.1.call-update) | async-done | bytes 2097168 | tf_op jit(solution)/shard_map/while/body/eval_jaxpr/all_gather | solution.py:8
  814.6 51.6 %all-gather.17.cloned.1.call-done = f32[4096,128]{1,0:T(8,128)} async-done(((f32[512,128]{1,0:T(8,128)}), f32[4096,128]{1,0:T(8,128)}) %all-gather.17.cloned.1.call-update) | async-done | bytes 2097168 | tf_op jit(solution)/shard_map/while/body/eval_jaxpr/all_gather | solution.py:8
  872.6 51.6 %all-gather.17.cloned.1.call-done = f32[4096,128]{1,0:T(8,128)} async-done(((f32[512,128]{1,0:T(8,128)}), f32[4096,128]{1,0:T(8,128)}) %all-gather.17.cloned.1.call-update) | async-done | bytes 2097168 | tf_op jit(solution)/shard_map/while/body/eval_jaxpr/all_gather | solution.py:8
  930.6 51.6 %all-gather.17.cloned.1.call-done = f32[4096,128]{1,0:T(8,128)} async-done(((f32[512,128]{1,0:T(8,128)}), f32[4096,128]{1,0:T(8,128)}) %all-gather.17.cloned.1.call-update) | async-done | bytes 2097168 | tf_op jit(solution)/shard_map/while/body/eval_jaxpr/all_gather | solution.py:8
  988.6 51.6 %all-gather.17.cloned.1.call-done = f32[4096,128]{1,0:T(8,128)} async-done(((f32[512,128]{1,0:T(8,128)}), f32[4096,128]{1,0:T(8,128)}) %all-gather.17.cloned.1.call-update) | async-done | bytes 2097168 | tf_op jit(solution)/shard_map/while/body/eval_jaxpr/all_gather | solution.py:8
  1046.6 51.6 %all-gather.17.cloned.1.call-done = f32[4096,128]{1,0:T(8,128)} async-done(((f32[512,128]{1,0:T(8,128)}), f32[4096,128]{1,0:T(8,128)}) %all-gather.17.cloned.1.call-update) | async-done | bytes 2097168 | tf_op jit(solution)/shard_map/while/body/eval_jaxpr/all_gather | solution.py:8
  1104.6 51.6 %all-gather.17.cloned.1.call-done = f32[4096,128]{1,0:T(8,128)} async-done(((f32[512,128]{1,0:T(8,128)}), f32[4096,128]{1,0:T(8,128)}) %all-gather.17.cloned.1.call-update) | async-done | bytes 2097168 | tf_op jit(solution)/shard_map/while/body/eval_jaxpr/all_gather | solution.py:8
  1162.6 51.6 %all-gather.17.cloned.1.call-done = f32[4096,128]{1,0:T(8,128)} async-done(((f32[512,128]{1,0:T(8,128)}), f32[4096,128]{1,0:T(8,128)}) %all-gather.17.cloned.1.call-update) | async-done | bytes 2097168 | tf_op jit(solution)/shard_map/while/body/eval_jaxpr/all_gather | solution.py:8
  (147 shorter events, 130.0 us)
Async XLA Ops:
  6.5 1.6 copy-start.1
  6.5 181.1 %all-gather.13.cloned.1.call-start = ((), (), s32[]{:S(2)}) async-start(), calls=%async_computation.2 | async-start | bytes 35651584 | tf_op jit(solution)/shard_map/all_gather | solution.py:54
  7.3 274.3 %all-gather.11.cloned.1.call-start = ((), (), s32[]{:S(2)}) async-start(), calls=%async_computation.1 | async-start | bytes 17825792 | tf_op jit(solution)/shard_map/all_gather | solution.py:55
  65.7 1.5 copy-start.2
  71.1 20.0 %all-to-all-start = ((f32[16,1,8192]{2,1,0:T(1,128)}), f32[16,1,8192]{2,1,0:T(1,128)S(1)}, u32[]{:S(2)}, u32[]{:S(2)}) async-start(f32[16,1,8192]{2,1,0:T(1,128)} %reshape.83), calls=%async_computation | async-start | bytes 1048576 | tf_op jit(solution)/shard_map/all_to_all | solution.py:20
  281.6 57.7 %all-gather.15.cloned.1.call-start = ((), (), s32[]{:S(2)}) async-start(), calls=%async_computation.3 | async-start | bytes 2359296 | tf_op jit(solution)/shard_map/while/body/eval_jaxpr/all_gather | solution.py:8
  343.3 54.6 %all-gather.15.cloned.1.call-start = ((), (), s32[]{:S(2)}) async-start(), calls=%async_computation.3 | async-start | bytes 2359296 | tf_op jit(solution)/shard_map/while/body/eval_jaxpr/all_gather | solution.py:8
  401.9 54.6 %all-gather.15.cloned.1.call-start = ((), (), s32[]{:S(2)}) async-start(), calls=%async_computation.3 | async-start | bytes 2359296 | tf_op jit(solution)/shard_map/while/body/eval_jaxpr/all_gather | solution.py:8
  460.5 54.6 %all-gather.15.cloned.1.call-start = ((), (), s32[]{:S(2)}) async-start(), calls=%async_computation.3 | async-start | bytes 2359296 | tf_op jit(solution)/shard_map/while/body/eval_jaxpr/all_gather | solution.py:8
  519.1 54.7 %all-gather.15.cloned.1.call-start = ((), (), s32[]{:S(2)}) async-start(), calls=%async_computation.3 | async-start | bytes 2359296 | tf_op jit(solution)/shard_map/while/body/eval_jaxpr/all_gather | solution.py:8
  577.7 54.6 %all-gather.15.cloned.1.call-start = ((), (), s32[]{:S(2)}) async-start(), calls=%async_computation.3 | async-start | bytes 2359296 | tf_op jit(solution)/shard_map/while/body/eval_jaxpr/all_gather | solution.py:8
  636.3 54.6 %all-gather.15.cloned.1.call-start = ((), (), s32[]{:S(2)}) async-start(), calls=%async_computation.3 | async-start | bytes 2359296 | tf_op jit(solution)/shard_map/while/body/eval_jaxpr/all_gather | solution.py:8
  694.9 54.6 %all-gather.15.cloned.1.call-start = ((), (), s32[]{:S(2)}) async-start(), calls=%async_computation.3 | async-start | bytes 2359296 | tf_op jit(solution)/shard_map/while/body/eval_jaxpr/all_gather | solution.py:8
  753.6 54.6 %all-gather.17.cloned.1.call-start = ((), (), s32[]{:S(2)}) async-start(), calls=%async_computation.4 | async-start | bytes 2359296 | tf_op jit(solution)/shard_map/while/body/eval_jaxpr/all_gather | solution.py:8
  811.6 54.6 %all-gather.17.cloned.1.call-start = ((), (), s32[]{:S(2)}) async-start(), calls=%async_computation.4 | async-start | bytes 2359296 | tf_op jit(solution)/shard_map/while/body/eval_jaxpr/all_gather | solution.py:8
  869.5 54.7 %all-gather.17.cloned.1.call-start = ((), (), s32[]{:S(2)}) async-start(), calls=%async_computation.4 | async-start | bytes 2359296 | tf_op jit(solution)/shard_map/while/body/eval_jaxpr/all_gather | solution.py:8
  927.6 54.6 %all-gather.17.cloned.1.call-start = ((), (), s32[]{:S(2)}) async-start(), calls=%async_computation.4 | async-start | bytes 2359296 | tf_op jit(solution)/shard_map/while/body/eval_jaxpr/all_gather | solution.py:8
  985.5 54.6 %all-gather.17.cloned.1.call-start = ((), (), s32[]{:S(2)}) async-start(), calls=%async_computation.4 | async-start | bytes 2359296 | tf_op jit(solution)/shard_map/while/body/eval_jaxpr/all_gather | solution.py:8
  1043.5 54.6 %all-gather.17.cloned.1.call-start = ((), (), s32[]{:S(2)}) async-start(), calls=%async_computation.4 | async-start | bytes 2359296 | tf_op jit(solution)/shard_map/while/body/eval_jaxpr/all_gather | solution.py:8
  1101.5 54.6 %all-gather.17.cloned.1.call-start = ((), (), s32[]{:S(2)}) async-start(), calls=%async_computation.4 | async-start | bytes 2359296 | tf_op jit(solution)/shard_map/while/body/eval_jaxpr/all_gather | solution.py:8
  1159.5 54.6 %all-gather.17.cloned.1.call-start = ((), (), s32[]{:S(2)}) async-start(), calls=%async_computation.4 | async-start | bytes 2359296 | tf_op jit(solution)/shard_map/while/body/eval_jaxpr/all_gather | solution.py:8
  1217.5 0.8 copy-start
Sparse Core Ops, SparseCore 0:
  9.0 178.6 all-gather.12
  189.3 92.2 all-gather.10
  284.7 54.5 all-gather.14
  346.4 51.4 all-gather.14
  405.0 51.4 all-gather.14
  463.6 51.4 all-gather.14
  522.2 51.4 all-gather.14
  580.9 51.4 all-gather.14
  639.5 51.4 all-gather.14
  698.1 51.4 all-gather.14
  756.7 51.4 all-gather.16
  814.7 51.4 all-gather.16
  872.7 51.4 all-gather.16
  930.7 51.4 all-gather.16
  988.7 51.4 all-gather.16
  1046.7 51.4 all-gather.16
  1104.7 51.4 all-gather.16
  1162.7 51.4 all-gather.16
where the time goes:
time: 1230 us
  waiting for transfers between devices  1000 us (81%)
  matrix products  94.2 us (8%)
  other arithmetic  59.8 us (5%)
  local copies, waits for them, and re-layouts  45.9 us (4%)
  between operations  13.6 us (1%)
    all_gather x16, waiting for transfers between devices, picked(): lax.all_gather(array, axis)  814 us
    all_gather x1, waiting for transfers between devices, on_device(): lax.all_gather(tri_panels, 'col', axis=1, tiled=True)  91.5 us
    all_gather x1, waiting for transfers between devices, on_device(): lax.all_gather(own_inverse, 'col', axis=1, tiled=True)  82.4 us
    dot_general x16, matrix products, advance(): jnp.dot(inverse_block, current, precision=lax.Precision.HIGHEST, preferre...  46.7 us
    dot_general x16, matrix products, advance(): jnp.einsum('sij,jc->sic', pieces, solution, precision=lax.Precision.HIGHEST)  41.8 us
    another operation x4, other arithmetic, on_device(): jax.scipy.linalg.solve_triangular(own_diag, identity_block, lower=True)  41.5 us
  transfers between devices with their start and end apart: 19, of which 19 were waited for; matrix products, arithmetic and copies ran while one was open for 8% of the time, Pallas kernels for 0%

commit v1 on v0

--- a/solution.py
+++ b/solution.py
@@ -50,9 +50,12 @@
         return trailing
 
     group_count = (col_count + row_count - 1) // row_count
+    watch_the_vectors = lambda u_in, axis_tag: jnp.concatenate(
+        lax.all_gather(u_in, axis_name=axis_tag), 1
+    )
     everything, inverses = (
         lax.all_gather(tri_panels, "col", axis=1, tiled=True),
-        lax.all_gather(own_inverse, "col", axis=1, tiled=True),
+        watch_the_vectors(own_inverse, "col"),
     )
     for first_slot in range(group_count):
         begin_step = first_slot * row_count

time: 1230 us -> 1290 us (1.049)
  waiting for transfers between devices: 1000 us -> 1060 us
    all_gather x1, waiting for transfers between devices: 91.5 us -> 161 us  [on_device(): lax.all_gather(tri_panels, 'col', axis=1, tiled=True)]
  transfers between devices with their start and end apart: 19 -> 19, of which waited for: 19 -> 19; matrix products, arithmetic and copies ran while one was open for 8% -> 3% of each run, Pallas kernels for 0% -> 0%
where the time goes in v1:
time: 1290 us
  waiting for transfers between devices  1060 us (82%)
  matrix products  91.5 us (7%)
  other arithmetic  60 us (5%)
  local copies, waits for them, and re-layouts  53.8 us (4%)
  between operations  13.6 us (1%)
    all_gather x16, waiting for transfers between devices, picked(): lax.all_gather(array, axis)  814 us
    all_gather x1, waiting for transfers between devices, on_device(): lax.all_gather(tri_panels, 'col', axis=1, tiled=True)  161 us
    all_gather x1, waiting for transfers between devices, on_device(): lax.all_gather(u_in, axis_name=axis_tag)  70.5 us
    dot_general x16, matrix products, advance(): jnp.dot(inverse_block, current, precision=lax.Precision.HIGHEST, preferre...  46.7 us
    dot_general x16, matrix products, advance(): jnp.einsum('sij,jc->sic', pieces, solution, precision=lax.Precision.HIGHEST)  41.8 us
    another operation x4, other arithmetic, on_device(): jax.scipy.linalg.solve_triangular(own_diag, identity_block, lower=True)  41.7 us
  transfers between devices with their start and end apart: 19, of which 19 were waited for; matrix products, arithmetic and copies ran while one was open for 3% of the time, Pallas kernels for 0%

profile of v1, /device:TPU:0, one launch (start us, length us, event | category | flops | bytes accessed | tf_op | source)
XLA Modules:
  0.0 1287.5 jit_solution(2364498989049787948)
XLA Ops:
  8.2 8.0 while.33
  16.2 39.3 %custom-call.4 = f32[4,128,128]{1,2,0:T(8,128)S(1)} custom-call(f32[4,128,128]{2,1,0:T(8,128)S(1)} %get-tuple-element.290), custom_call_target="InvertDiagBlocksLowerTriangular" | custom-call | tf_op jit(solution)/shard_map/jit(_solve_triangular)/triangular_solve | solution.py:25
  64.6 5.5 all-to-all-start
  70.1 13.7 %all-to-all-done = f32[16,1,8192]{2,1,0:T(1,128)S(1)} async-done(((f32[16,1,8192]{2,1,0:T(1,128)}), f32[16,1,8192]{2,1,0:T(1,128)S(1)}, u32[]{:S(2)}, u32[]{:S(2)}) %all-to-all-start) | async-done | bytes 524320 | tf_op jit(solution)/shard_map/all_to_all | solution.py:20
  88.9 70.5 %all-gather.14.cloned.1.call-done = f32[8192,512]{1,0:T(8,128)} async-done(((f32[512,512]{1,0:T(8,128)}), f32[8192,512]{1,0:T(8,128)}) %all-gather.14.cloned.1.call-update) | async-done | bytes 16777232 | tf_op jit(solution)/shard_map/all_gather | solution.py:54
  159.3 12.0 copy.17
  171.3 161.2 %all-gather.12.cloned.1.call-done = f32[1024,8192]{1,0:T(8,128)} async-done(((f32[1024,512]{1,0:T(8,128)}), f32[1024,8192]{1,0:T(8,128)}) %all-gather.12.cloned.1.call-update) | async-done | bytes 33554448 | tf_op jit(solution)/shard_map/all_gather | solution.py:57
  332.5 11.5 slice.70
  344.0 471.8 %while.31 = (s32[]{:T(128)}, f32[2,512,128]{2,1,0:T(8,128)S(1)}, s32[]{:T(128)}, f32[512,8192]{1,0:T(8,128)}, f32[1024,8192]{1,0:T(8,128)}, /*index=5*/s32[]{:T(...) while((s32[]{:T(128)}, f32[2,512,128]{2,1,0:T(8,128)S(1)}, ...), condition=%wide.region_1.2_spmd, body=%wide.region_0.1_spmd.sunk | while | flops 1208287232 | bytes 17039816 | solution.py:72
  348.7 52.9 %all-gather.16.cloned.1.call-done = f32[4096,128]{1,0:T(8,128)} async-done(((f32[512,128]{1,0:T(8,128)}), f32[4096,128]{1,0:T(8,128)}) %all-gather.16.cloned.1.call-update) | async-done | bytes 2097168 | tf_op jit(solution)/shard_map/while/body/eval_jaxpr/all_gather | solution.py:8
  410.4 49.8 %all-gather.16.cloned.1.call-done = f32[4096,128]{1,0:T(8,128)} async-done(((f32[512,128]{1,0:T(8,128)}), f32[4096,128]{1,0:T(8,128)}) %all-gather.16.cloned.1.call-update) | async-done | bytes 2097168 | tf_op jit(solution)/shard_map/while/body/eval_jaxpr/all_gather | solution.py:8
  461.2 3.0 fusion.64
  469.0 49.8 %all-gather.16.cloned.1.call-done = f32[4096,128]{1,0:T(8,128)} async-done(((f32[512,128]{1,0:T(8,128)}), f32[4096,128]{1,0:T(8,128)}) %all-gather.16.cloned.1.call-update) | async-done | bytes 2097168 | tf_op jit(solution)/shard_map/while/body/eval_jaxpr/all_gather | solution.py:8
  519.8 3.0 fusion.64
  527.6 49.8 %all-gather.16.cloned.1.call-done = f32[4096,128]{1,0:T(8,128)} async-done(((f32[512,128]{1,0:T(8,128)}), f32[4096,128]{1,0:T(8,128)}) %all-gather.16.cloned.1.call-update) | async-done | bytes 2097168 | tf_op jit(solution)/shard_map/while/body/eval_jaxpr/all_gather | solution.py:8
  578.4 3.0 fusion.64
  586.2 49.8 %all-gather.16.cloned.1.call-done = f32[4096,128]{1,0:T(8,128)} async-done(((f32[512,128]{1,0:T(8,128)}), f32[4096,128]{1,0:T(8,128)}) %all-gather.16.cloned.1.call-update) | async-done | bytes 2097168 | tf_op jit(solution)/shard_map/while/body/eval_jaxpr/all_gather | solution.py:8
  637.0 3.0 fusion.64
  644.8 49.8 %all-gather.16.cloned.1.call-done = f32[4096,128]{1,0:T(8,128)} async-done(((f32[512,128]{1,0:T(8,128)}), f32[4096,128]{1,0:T(8,128)}) %all-gather.16.cloned.1.call-update) | async-done | bytes 2097168 | tf_op jit(solution)/shard_map/while/body/eval_jaxpr/all_gather | solution.py:8
  695.6 3.0 fusion.64
  703.4 49.8 %all-gather.16.cloned.1.call-done = f32[4096,128]{1,0:T(8,128)} async-done(((f32[512,128]{1,0:T(8,128)}), f32[4096,128]{1,0:T(8,128)}) %all-gather.16.cloned.1.call-update) | async-done | bytes 2097168 | tf_op jit(solution)/shard_map/while/body/eval_jaxpr/all_gather | solution.py:8
  762.1 49.8 %all-gather.16.cloned.1.call-done = f32[4096,128]{1,0:T(8,128)} async-done(((f32[512,128]{1,0:T(8,128)}), f32[4096,128]{1,0:T(8,128)}) %all-gather.16.cloned.1.call-update) | async-done | bytes 2097168 | tf_op jit(solution)/shard_map/while/body/eval_jaxpr/all_gather | solution.py:8
  812.9 3.0 fusion.64
  815.8 464.0 %while.32 = (s32[]{:T(128)}, f32[2,512,128]{2,1,0:T(8,128)S(1)}, s32[]{:T(128)}, f32[512,8192]{1,0:T(8,128)}, s32[1]{0:T(128)}, /*index=5*/f32[512,8192]{1,0:T(8...) while((s32[]{:T(128)}, f32[2,512,128]{2,1,0:T(8,128)S(1)}, ...), condition=%wide.region_3.4_spmd, body=%wide.region_2.3_spmd.sunk | while | flops 805634048 | bytes 12846105 | solution.py:72
  818.9 51.6 %all-gather.18.cloned.1.call-done = f32[4096,128]{1,0:T(8,128)} async-done(((f32[512,128]{1,0:T(8,128)}), f32[4096,128]{1,0:T(8,128)}) %all-gather.18.cloned.1.call-update) | async-done | bytes 2097168 | tf_op jit(solution)/shard_map/while/body/eval_jaxpr/all_gather | solution.py:8
  876.9 51.6 %all-gather.18.cloned.1.call-done = f32[4096,128]{1,0:T(8,128)} async-done(((f32[512,128]{1,0:T(8,128)}), f32[4096,128]{1,0:T(8,128)}) %all-gather.18.cloned.1.call-update) | async-done | bytes 2097168 | tf_op jit(solution)/shard_map/while/body/eval_jaxpr/all_gather | solution.py:8
  934.9 51.6 %all-gather.18.cloned.1.call-done = f32[4096,128]{1,0:T(8,128)} async-done(((f32[512,128]{1,0:T(8,128)}), f32[4096,128]{1,0:T(8,128)}) %all-gather.18.cloned.1.call-update) | async-done | bytes 2097168 | tf_op jit(solution)/shard_map/while/body/eval_jaxpr/all_gather | solution.py:8
  992.9 51.6 %all-gather.18.cloned.1.call-done = f32[4096,128]{1,0:T(8,128)} async-done(((f32[512,128]{1,0:T(8,128)}), f32[4096,128]{1,0:T(8,128)}) %all-gather.18.cloned.1.call-update) | async-done | bytes 2097168 | tf_op jit(solution)/shard_map/while/body/eval_jaxpr/all_gather | solution.py:8
  1050.9 51.6 %all-gather.18.cloned.1.call-done = f32[4096,128]{1,0:T(8,128)} async-done(((f32[512,128]{1,0:T(8,128)}), f32[4096,128]{1,0:T(8,128)}) %all-gather.18.cloned.1.call-update) | async-done | bytes 2097168 | tf_op jit(solution)/shard_map/while/body/eval_jaxpr/all_gather | solution.py:8
  1108.9 51.6 %all-gather.18.cloned.1.call-done = f32[4096,128]{1,0:T(8,128)} async-done(((f32[512,128]{1,0:T(8,128)}), f32[4096,128]{1,0:T(8,128)}) %all-gather.18.cloned.1.call-update) | async-done | bytes 2097168 | tf_op jit(solution)/shard_map/while/body/eval_jaxpr/all_gather | solution.py:8
  1166.9 51.6 %all-gather.18.cloned.1.call-done = f32[4096,128]{1,0:T(8,128)} async-done(((f32[512,128]{1,0:T(8,128)}), f32[4096,128]{1,0:T(8,128)}) %all-gather.18.cloned.1.call-update) | async-done | bytes 2097168 | tf_op jit(solution)/shard_map/while/body/eval_jaxpr/all_gather | solution.py:8
  1224.9 51.6 %all-gather.18.cloned.1.call-done = f32[4096,128]{1,0:T(8,128)} async-done(((f32[512,128]{1,0:T(8,128)}), f32[4096,128]{1,0:T(8,128)}) %all-gather.18.cloned.1.call-update) | async-done | bytes 2097168 | tf_op jit(solution)/shard_map/while/body/eval_jaxpr/all_gather | solution.py:8
  (146 shorter events, 126.4 us)
Async XLA Ops:
  6.5 152.8 %all-gather.14.cloned.1.call-start = ((), (), s32[]{:S(2)}) async-start(), calls=%async_computation.2 | async-start | bytes 17825792 | tf_op jit(solution)/shard_map/all_gather | solution.py:54
  59.7 1.0 copy-start.1
  59.7 272.8 %all-gather.12.cloned.1.call-start = ((), (), s32[]{:S(2)}) async-start(), calls=%async_computation.1 | async-start | bytes 35651584 | tf_op jit(solution)/shard_map/all_gather | solution.py:57
  64.6 19.2 %all-to-all-start = ((f32[16,1,8192]{2,1,0:T(1,128)}), f32[16,1,8192]{2,1,0:T(1,128)S(1)}, u32[]{:S(2)}, u32[]{:S(2)}) async-start(f32[16,1,8192]{2,1,0:T(1,128)} %reshape.92), calls=%async_computation | async-start | bytes 1048576 | tf_op jit(solution)/shard_map/all_to_all | solution.py:20
  344.0 57.6 %all-gather.16.cloned.1.call-start = ((), (), s32[]{:S(2)}) async-start(), calls=%async_computation.3 | async-start | bytes 2359296 | tf_op jit(solution)/shard_map/while/body/eval_jaxpr/all_gather | solution.py:8
  405.6 54.6 %all-gather.16.cloned.1.call-start = ((), (), s32[]{:S(2)}) async-start(), calls=%async_computation.3 | async-start | bytes 2359296 | tf_op jit(solution)/shard_map/while/body/eval_jaxpr/all_gather | solution.py:8
  464.2 54.6 %all-gather.16.cloned.1.call-start = ((), (), s32[]{:S(2)}) async-start(), calls=%async_computation.3 | async-start | bytes 2359296 | tf_op jit(solution)/shard_map/while/body/eval_jaxpr/all_gather | solution.py:8
  522.8 54.6 %all-gather.16.cloned.1.call-start = ((), (), s32[]{:S(2)}) async-start(), calls=%async_computation.3 | async-start | bytes 2359296 | tf_op jit(solution)/shard_map/while/body/eval_jaxpr/all_gather | solution.py:8
  581.4 54.7 %all-gather.16.cloned.1.call-start = ((), (), s32[]{:S(2)}) async-start(), calls=%async_computation.3 | async-start | bytes 2359296 | tf_op jit(solution)/shard_map/while/body/eval_jaxpr/all_gather | solution.py:8
  640.0 54.6 %all-gather.16.cloned.1.call-start = ((), (), s32[]{:S(2)}) async-start(), calls=%async_computation.3 | async-start | bytes 2359296 | tf_op jit(solution)/shard_map/while/body/eval_jaxpr/all_gather | solution.py:8
  698.6 54.6 %all-gather.16.cloned.1.call-start = ((), (), s32[]{:S(2)}) async-start(), calls=%async_computation.3 | async-start | bytes 2359296 | tf_op jit(solution)/shard_map/while/body/eval_jaxpr/all_gather | solution.py:8
  757.2 54.6 %all-gather.16.cloned.1.call-start = ((), (), s32[]{:S(2)}) async-start(), calls=%async_computation.3 | async-start | bytes 2359296 | tf_op jit(solution)/shard_map/while/body/eval_jaxpr/all_gather | solution.py:8
  815.9 54.6 %all-gather.18.cloned.1.call-start = ((), (), s32[]{:S(2)}) async-start(), calls=%async_computation.4 | async-start | bytes 2359296 | tf_op jit(solution)/shard_map/while/body/eval_jaxpr/all_gather | solution.py:8
  873.9 54.6 %all-gather.18.cloned.1.call-start = ((), (), s32[]{:S(2)}) async-start(), calls=%async_computation.4 | async-start | bytes 2359296 | tf_op jit(solution)/shard_map/while/body/eval_jaxpr/all_gather | solution.py:8
  931.8 54.7 %all-gather.18.cloned.1.call-start = ((), (), s32[]{:S(2)}) async-start(), calls=%async_computation.4 | async-start | bytes 2359296 | tf_op jit(solution)/shard_map/while/body/eval_jaxpr/all_gather | solution.py:8
  989.9 54.6 %all-gather.18.cloned.1.call-start = ((), (), s32[]{:S(2)}) async-start(), calls=%async_computation.4 | async-start | bytes 2359296 | tf_op jit(solution)/shard_map/while/body/eval_jaxpr/all_gather | solution.py:8
  1047.8 54.6 %all-gather.18.cloned.1.call-start = ((), (), s32[]{:S(2)}) async-start(), calls=%async_computation.4 | async-start | bytes 2359296 | tf_op jit(solution)/shard_map/while/body/eval_jaxpr/all_gather | solution.py:8
  1105.8 54.6 %all-gather.18.cloned.1.call-start = ((), (), s32[]{:S(2)}) async-start(), calls=%async_computation.4 | async-start | bytes 2359296 | tf_op jit(solution)/shard_map/while/body/eval_jaxpr/all_gather | solution.py:8
  1163.8 54.6 %all-gather.18.cloned.1.call-start = ((), (), s32[]{:S(2)}) async-start(), calls=%async_computation.4 | async-start | bytes 2359296 | tf_op jit(solution)/shard_map/while/body/eval_jaxpr/all_gather | solution.py:8
  1221.8 54.6 %all-gather.18.cloned.1.call-start = ((), (), s32[]{:S(2)}) async-start(), calls=%async_computation.4 | async-start | bytes 2359296 | tf_op jit(solution)/shard_map/while/body/eval_jaxpr/all_gather | solution.py:8
  1279.8 0.8 copy-start
Sparse Core Ops, SparseCore 0:
  59.8 99.4 all-gather.13
  161.0 171.4 all-gather.11
  347.1 54.4 all-gather.15
  408.7 51.4 all-gather.15
  467.3 51.4 all-gather.15
  525.9 51.4 all-gather.15
  584.5 51.4 all-gather.15
  643.2 51.4 all-gather.15
  701.8 51.4 all-gather.15
  760.4 51.4 all-gather.15
  819.0 51.4 all-gather.17
  877.0 51.4 all-gather.17
  935.0 51.4 all-gather.17
  993.0 51.4 all-gather.17
  1051.0 51.4 all-gather.17
  1109.0 51.4 all-gather.17
  1167.0 51.4 all-gather.17
  1225.0 51.4 all-gather.17
